TPU v7x, 32 devices: a whole 2x2x4 slice. The times are simulated.
32 devices in a mesh: groups: 2 (over x), freq: 8 (over z, y), gvec: 2 (over core).
Axes of the slice: x: 2, y: 2, z: 4, core: 2. Of those that a mesh axis runs over, the one named last changes fastest.
Arguments:
- screened: bfloat16 [16, 3072, 3072], P(('groups', 'freq'), 'gvec'), parts along dimension 0, may hold values from -0.109375 to 0.109375
- densities: bfloat16 [6144, 512], P(('groups', 'gvec'), 'freq'), parts along dimension 0, may hold values from -0.8046875 to 0.8046875
- pair_order: int32 [512], replicated, may hold values from 0 to 511, each once
- quad_index: int32 [4, 8], replicated, may hold values from 0 to 63
- quad_table: float32 [64], replicated, may hold values from 0.05 to 0.5
Outputs:
- kernel_out: float32 [8, 512, 512], P('groups', 'freq', 'gvec'), parts along dimension 0
There are 2 independent parts, one for each index of `groups`. A program takes and returns all parts, laid end to end along the dimension named above; an argument that names none is the same for every part. Nothing has to cross between parts.
All inputs are finite; a program needn't handle non-finite values.
Results may differ from a plain program's by a relative error of at most 0.0029.
Values may be sent and summed in bfloat16 or wider, within the bound.
A program may use at most 64 MiB of HBM per device.

v0:
```python
import functools

import jax
import jax.numpy as jnp
from jax import lax
from jax.experimental import pallas as pl
from jax.experimental.pallas import tpu as pltpu
from jax.sharding import PartitionSpec as P

MESH = pl.DeviceIdType.MESH
F32 = jnp.float32
BF16 = jnp.bfloat16
NT = (((1,), (1,)), ((), ()))


def kernel(
    n, chunks, screened, dens, order, quad_index, quad_table, out,
    w_buf, x_buf, e_buf, acc, pa_buf, p_buf, perm, order_rows, k_send, k_peer, k_own, k_red, rows_in,
    own_sem, w_sem, ring_send, ring_recv, pair_send, pair_recv, half_send, half_recv, out_send, out_recv,
):
    per, rows = dens.shape
    pairs = n * per
    half = pairs // 2
    mid = n // 2
    width = rows // chunks
    me = lax.axis_index("freq")
    core = lax.axis_index("gvec")
    peer = 1 - core

    def index_at(position):
        fold = position // mid
        return (1 - fold) * (2 * position) + fold * (2 * (n - 1 - position) + 1)

    odd = me % 2
    place = (1 - odd) * (me // 2) + odd * (n - 1 - me // 2)
    right = index_at((place + 1) % n)
    left = index_at((place + n - 1) % n)

    barrier = pltpu.get_barrier_semaphore()
    pl.semaphore_signal(barrier, inc=1, device_id={"freq": left}, device_id_type=MESH)
    pl.semaphore_signal(barrier, inc=1, device_id={"freq": right}, device_id_type=MESH)
    pl.semaphore_signal(barrier, inc=1, device_id={"gvec": peer}, device_id_type=MESH)

    def w_copy(c, h):
        columns = pl.ds(h * rows + c * width, width)
        return pltpu.make_async_copy(
            screened.at[0, :, columns], w_buf.at[c, h], w_sem.at[c, h]
        )

    mine = pl.ds(pl.multiple_of(me * per, per), per)

    def own_copy(c):
        return pltpu.make_async_copy(
            dens.at[:, pl.ds(c * width, width)], x_buf.at[c, core, 0:per, :], own_sem.at[c]
        )

    for c in range(chunks):
        own_copy(c).start()

    def spot(d, side):
        return n - 1 if d == mid else max(0, 2 * d - 1 + side)

    def ring_copy(c, d, side, target):
        return pltpu.make_async_remote_copy(
            src_ref=x_buf.at[c, core, pl.ds(spot(d, side) * per, per), :],
            dst_ref=x_buf.at[c, core, pl.ds(spot(d + 1, side) * per, per), :],
            send_sem=ring_send.at[c, side * mid + d], recv_sem=ring_recv.at[c, side * mid + d],
            device_id={"freq": target}, device_id_type=MESH,
        )

    def pair_copy(c, at, core_from):
        ref = x_buf.at[c, core_from, pl.ds(at * per, per), :]
        return pltpu.make_async_remote_copy(
            src_ref=ref, dst_ref=ref, send_sem=pair_send.at[c, at],
            recv_sem=pair_recv.at[c, at], device_id={"gvec": peer}, device_id_type=MESH,
        )

    def reach(c):
        ahead = mid if c % 2 == 0 else mid - 1
        return ahead, n - 1 - ahead

    for c in range(chunks):
        own_copy(c).wait()
    pl.semaphore_wait(barrier, 3)
    for c in range(chunks):
        ring_copy(c, 0, 0, right).start()
        ring_copy(c, 0, 1, left).start()
    for c in range(chunks):
        pair_copy(c, 0, core).start()
    for c in range(chunks):
        for h in range(2):
            w_copy(c, h).start()

    for at in range(n):
        d, side = (at + 1) // 2, 1 - at % 2
        origin = index_at((place + (d if side else n - d)) % n)
        pair = lax.broadcasted_iota(jnp.int32, (per, pairs), 0) + origin * per
        one_hot = (pair == order[...]).astype(F32)
        order_rows[at * per:(at + 1) * per, :] = one_hot.astype(BF16)
    perm[...] = order_rows[...].astype(F32).T.astype(BF16)

    def take(c, d):
        for side, last, target in zip((0, 1), reach(c), (right, left)):
            if d <= last:
                ring_copy(c, d - 1, side, target).wait_recv()
                if d < last:
                    ring_copy(c, d, side, target).start()
                pair_copy(c, spot(d, side), core).start()

    tile = rows // 2 if rows % 32 == 0 else rows

    def multiply(c, g):
        for at in range(g * mid, (g + 1) * mid):
            pair_copy(c, at, peer).wait_recv()
        if g == 0:
            for h in range(2):
                w_copy(c, h).wait()
        members = slice(g * half, (g + 1) * half)

        def step(t, _):
            at = pl.ds(pl.multiple_of(t * tile, tile), tile)
            total = sum(
                lax.dot_general(
                    w_buf[c, h, at, :], x_buf[c, h, members, :], NT,
                    preferred_element_type=F32,
                )
                for h in range(2)
            )
            if c > 0:
                total = total + acc[g, at, :]
            if c < chunks - 1:
                acc[g, at, :] = total
                return 0
            total = total.astype(BF16)
            for h in range(2):
                part = jnp.dot(
                    total, order_rows[members, h * half:(h + 1) * half],
                    preferred_element_type=F32,
                )
                if g == 0:
                    pa_buf[h, at, :] = part.astype(BF16)
                else:
                    p_buf[h, at, :] = (part + pa_buf[h, at, :].astype(F32)).astype(BF16)
            return 0

        lax.fori_loop(0, rows // tile, step, 0)

    def order_own(c):
        e_buf[:, c * width:(c + 1) * width] = jnp.dot(
            perm[...], x_buf[c, core], preferred_element_type=F32
        ).astype(BF16)

    for d in range(1, mid // 2 + 1):
        for c in range(chunks):
            take(c, d)
    for c in range(chunks):
        multiply(c, 0)
        for d in range(mid // 2 + 1, mid):
            take(c, d)
    for c in range(chunks):
        take(c, mid)
    for c in range(chunks):
        order_own(c)
        multiply(c, 1)

    def half_copy(i):
        return pltpu.make_async_remote_copy(
            src_ref=k_send.at[i], dst_ref=k_peer.at[i], send_sem=half_send.at[i],
            recv_sem=half_recv.at[i], device_id={"gvec": peer}, device_id_type=MESH,
        )

    def out_copy(target, slot):
        return pltpu.make_async_remote_copy(
            src_ref=k_red.at[pl.ds(pl.multiple_of(target * per, per), per), :],
            dst_ref=rows_in.at[me], send_sem=out_send.at[slot], recv_sem=out_recv.at[me],
            device_id={"freq": target}, device_id_type=MESH,
        )

    near = me // mid
    blocks = (1 - near, near)
    local = me % mid

    for i, b in enumerate(blocks):
        at = pl.ds(pl.multiple_of(b * half, half), half)
        k_send[i] = jnp.dot(e_buf[at, :], p_buf[peer], preferred_element_type=F32)
        half_copy(i).start()
    for i, b in enumerate(blocks):
        at = pl.ds(pl.multiple_of(b * half, half), half)
        k_own[i] = jnp.dot(e_buf[at, :], p_buf[core], preferred_element_type=F32)
    targets = []
    for i, b in enumerate(blocks):
        at = pl.ds(pl.multiple_of(b * half, half), half)
        half_copy(i).wait_recv()
        k_red[at, :] = (k_own[i] + k_peer[i]).astype(BF16)
        for t in range(i, mid):
            target = b * mid + (local + t) % mid
            out_copy(target, len(targets)).start()
            targets.append(target)
    rows_in[me] = k_red[mine, :]

    for t in range(1, n):
        source = (me + t) % n
        pltpu.make_async_remote_copy(
            src_ref=rows_in.at[source], dst_ref=rows_in.at[source],
            send_sem=out_send.at[0], recv_sem=out_recv.at[source],
            device_id={"freq": source}, device_id_type=MESH,
        ).wait_recv()
    for o in range(out.shape[0]):
        out[o] = sum(
            quad_table[quad_index[o, f]] * rows_in[f].astype(F32) for f in range(n)
        )

    for c in range(chunks):
        for side, last, target in zip((0, 1), reach(c), (right, left)):
            for d in range(last):
                ring_copy(c, d, side, target).wait_send()
        for at in range(n):
            pair_copy(c, at, core).wait_send()
    for i in range(2):
        half_copy(i).wait_send()
    for slot, target in enumerate(targets):
        out_copy(target, slot).wait_send()


def body(n, screened, densities, pair_order, quad_index, quad_table):
    rows, per = densities.shape
    pairs = n * per
    half = pairs // 2
    chunks = next(c for c in (4, 3, 2, 1) if rows % (c * 128) == 0 or c == 1)
    width = rows // chunks
    energies = quad_index.shape[0]
    dma = pltpu.SemaphoreType.DMA
    hbm = pl.BlockSpec(memory_space=pl.ANY)
    vmem = pl.BlockSpec(memory_space=pltpu.VMEM)
    smem = pl.BlockSpec(memory_space=pltpu.SMEM)
    return pl.pallas_call(
        functools.partial(kernel, n, chunks),
        out_shape=jax.ShapeDtypeStruct((energies, per, half), F32),
        in_specs=[hbm, hbm, vmem, smem, smem],
        out_specs=vmem,
        scratch_shapes=[
            pltpu.VMEM((chunks, 2, rows, width), BF16),
            pltpu.VMEM((chunks, 2, pairs, width), BF16),
            pltpu.VMEM((pairs, rows), BF16),
            pltpu.VMEM((2, rows, half), F32),
            pltpu.VMEM((2, rows, half), BF16),
            pltpu.VMEM((2, rows, half), BF16),
            pltpu.VMEM((pairs, pairs), BF16),
            pltpu.VMEM((pairs, pairs), BF16),
            pltpu.VMEM((2, half, half), F32),
            pltpu.VMEM((2, half, half), F32),
            pltpu.VMEM((2, half, half), F32),
            pltpu.VMEM((pairs, half), BF16),
            pltpu.VMEM((n, per, half), BF16),
            dma((chunks,)), dma((chunks, 2)),
            dma((chunks, n)), dma((chunks, n)),
            dma((chunks, n)), dma((chunks, n)),
            dma((2,)), dma((2,)), dma((n,)), dma((n,)),
        ],
        compiler_params=pltpu.CompilerParams(
            collective_id=0, has_side_effects=True, vmem_limit_bytes=60 * 1024 * 1024
        ),
    )(screened, densities.T, pair_order[None, :], quad_index, quad_table)


def solution(mesh):
    placed = (P(("groups", "freq"), "gvec", None), P(("groups", "gvec"), "freq"), P(), P(), P())
    return jax.shard_map(
        functools.partial(body, mesh.shape["freq"]), mesh=mesh, in_specs=placed,
        out_specs=P("groups", "freq", "gvec"), check_vma=False,
    )
```

profile of v0, /device:TPU:0, one launch (start us, length us, event | category | flops | bytes accessed | tf_op | source)
XLA Modules:
  0.0 47.4 jit_solution(8076514751275478089)
XLA Ops:
  0.0 45.7 %shard_map.55 = f32[4,64,256]{2,1,0:T(8,128)} custom-call(bf16[1,1536,3072]{2,1,0:T(8,128)(2,1)} %screened.1, bf16[64,1536]{1,0:T(8,128)(2,1)} %bitcast.2, s32[1,512]{1,0:T(1,128)} %bitcast.3, s32[4,8]{1,0:T(4,128)} %quad_index.1, f32[64]{0:T(128)} %quad_table.1), custom_call_target="tpu_custom_call" | custom-call | tf_op jit(solution)/shard_map/pallas_call | solution.py:236
  45.7 1.7 %copy.7 = f32[4,64,256]{2,1,0:T(8,128)} copy(f32[4,64,256]{2,1,0:T(8,128)} %shard_map.55) | data formatting | bytes 524288
where the time goes:
time: 47.6 us; the launch traced here: 47.4 us
  Pallas kernels  45.7 us (96%)
  local copies, waits for them, and re-layouts  1.67 us (4%)
    pallas_call x1, Pallas kernels, body(): pl.pallas_call(functools.partial(kernel, n, chunks), out_shape=jax.ShapeD...  45.7 us
    unnamed x1, local copies, waits for them, and re-layouts  1.67 us

commit v1 on v0

v1 whole, which is shorter than its diff:
```python
import functools

import jax
import jax.numpy as jnp
from jax import lax
from jax.experimental import pallas as pl
from jax.experimental.pallas import tpu as pltpu
from jax.sharding import PartitionSpec as P

MESH = pl.DeviceIdType.MESH
F32 = jnp.float32
BF16 = jnp.bfloat16
NT = (((1,), (1,)), ((), ()))


def kernel(
    n, chunks, screened, dens, order, quad_index, quad_table, out,
    w_buf, x_buf, e_buf, acc, pa_buf, p_buf, perm, order_rows, k_send, k_peer, k_own, k_red, rows_in,
    own_sem, w_sem, ring_send, ring_recv, own_send, own_recv, pair_send, pair_recv,
    half_send, half_recv, out_send, out_recv,
):
    per, rows = dens.shape
    pairs = n * per
    half = pairs // 2
    mid = n // 2
    width = rows // chunks
    me = lax.axis_index("freq")
    core = lax.axis_index("gvec")
    peer = 1 - core

    def index_at(position):
        fold = position // mid
        return (1 - fold) * (2 * position) + fold * (2 * (n - 1 - position) + 1)

    odd = me % 2
    place = (1 - odd) * (me // 2) + odd * (n - 1 - me // 2)
    right = index_at((place + 1) % n)
    left = index_at((place + n - 1) % n)

    own_copy = pltpu.make_async_copy(dens, x_buf.at[core, 0:per, :], own_sem.at[0])
    own_copy.start()

    barrier = pltpu.get_barrier_semaphore()
    pl.semaphore_signal(barrier, inc=1, device_id={"freq": left}, device_id_type=MESH)
    pl.semaphore_signal(barrier, inc=1, device_id={"freq": right}, device_id_type=MESH)
    pl.semaphore_signal(barrier, inc=1, device_id={"gvec": peer}, device_id_type=MESH)

    def w_copy(h):
        return pltpu.make_async_copy(
            screened.at[0, :, pl.ds(h * rows, rows)], w_buf.at[h], w_sem.at[h]
        )

    mine = pl.ds(pl.multiple_of(me * per, per), per)

    def lanes(c, count=1):
        return pl.ds(c * width, count * width)

    def spot(d, side):
        return n - 1 if d == mid else max(0, 2 * d - 1 + side)

    def block(c, at, half_of):
        return x_buf.at[half_of, pl.ds(at * per, per), lanes(c)]

    def ring_copy(c, d, side):
        return pltpu.make_async_remote_copy(
            src_ref=block(c, spot(d, side), core), dst_ref=block(c, spot(d + 1, side), core),
            send_sem=ring_send.at[c, side * mid + d], recv_sem=ring_recv.at[c, side * mid + d],
            device_id={"freq": left if side else right}, device_id_type=MESH,
        )

    def pair_copy(c, at, half_of):
        ref = block(c, at, half_of)
        return pltpu.make_async_remote_copy(
            src_ref=ref, dst_ref=ref, send_sem=pair_send.at[c, at],
            recv_sem=pair_recv.at[c, at], device_id={"gvec": peer}, device_id_type=MESH,
        )

    def own_pair(half_of):
        ref = x_buf.at[half_of, 0:per, :]
        return pltpu.make_async_remote_copy(
            src_ref=ref, dst_ref=ref, send_sem=own_send.at[0],
            recv_sem=own_recv.at[0], device_id={"gvec": peer}, device_id_type=MESH,
        )

    evens, odds = list(range(0, chunks, 2)), list(range(1, chunks, 2))
    sequence = (evens + odds, odds + evens)

    def reach(c, side):
        return mid if c % 2 == side else mid - 1

    own_copy.wait()
    pl.semaphore_wait(barrier, 3)
    for i in range(chunks):
        for side in range(2):
            ring_copy(sequence[side][i], 0, side).start()
    own_pair(core).start()
    for h in range(2):
        w_copy(h).start()

    for at in range(n):
        d, side = (at + 1) // 2, 1 - at % 2
        origin = index_at((place + (d if side else n - d)) % n)
        pair = lax.broadcasted_iota(jnp.int32, (per, pairs), 0) + origin * per
        one_hot = (pair == order[...]).astype(F32)
        order_rows[at * per:(at + 1) * per, :] = one_hot.astype(BF16)
    perm[...] = order_rows[...].astype(F32).T.astype(BF16)

    groups = (slice(0, half), slice(half, pairs))
    joined = 2 if chunks % 2 == 0 else 1
    spans = [lanes(c, joined) for c in range(0, chunks, joined)]
    seen = set()

    def have(g, j):
        for at in range(g * mid, (g + 1) * mid):
            for c in range(j * joined, (j + 1) * joined):
                key = (0, 0) if at == 0 else (c, at)
                if key not in seen:
                    seen.add(key)
                    if at == 0:
                        own_pair(peer).wait_recv()
                    else:
                        pair_copy(c, at, peer).wait_recv()

    def have_w():
        if "w" not in seen:
            seen.add("w")
            for h in range(2):
                w_copy(h).wait()

    tile = rows // 2 if rows % 32 == 0 else rows
    tiles = [slice(r, r + tile) for r in range(0, rows, tile)]

    def term(g, j, h, at):
        return lax.dot_general(
            w_buf[h, at, spans[j]], x_buf[h, groups[g], spans[j]], NT, preferred_element_type=F32
        )

    def turned(g, at, total):
        total = total.astype(BF16)
        for h in range(2):
            part = jnp.dot(
                total, order_rows[groups[g], h * half:(h + 1) * half], preferred_element_type=F32
            )
            if g == 0:
                pa_buf[h, at, :] = part.astype(BF16)
            else:
                p_buf[h, at, :] = (part + pa_buf[h, at, :].astype(F32)).astype(BF16)

    def early(j, at):
        def run():
            have_w()
            have(0, j)
            total = term(0, j, 0, at) + term(0, j, 1, at)
            if j > 0:
                total = total + acc[0, at, :]
            if j < len(spans) - 1:
                acc[0, at, :] = total
            else:
                turned(0, at, total)
        return run

    def late_own(j):
        def run():
            have_w()
            for at in tiles:
                total = term(1, j, core, at)
                if j > 0:
                    total = total + acc[1, at, :]
                acc[1, at, :] = total
        return run

    def late_peer(j):
        def run():
            have(1, j)
            for at in tiles:
                total = acc[1, at, :] + term(1, j, peer, at)
                if j < len(spans) - 1:
                    acc[1, at, :] = total
                else:
                    turned(1, at, total)
        return run

    def order_own(g, j):
        def run():
            part = jnp.dot(
                perm[:, groups[g]], x_buf[core, groups[g], spans[j]], preferred_element_type=F32
            )
            if g == 1:
                part = part + e_buf[:, spans[j]].astype(F32)
            e_buf[:, spans[j]] = part.astype(BF16)
        return run

    def arrival(j, d, side):
        return max(
            (d - 1) * chunks + sequence[side].index(c)
            for c in range(j * joined, (j + 1) * joined) if c % 2 == side or d < mid
        )

    todo = []
    turn = mid // 2
    for j in range(len(spans)):
        for at in tiles:
            todo.append((arrival(j, turn, 0) + 1, early(j, at)))
    for j in range(len(spans)):
        todo.append((arrival(j, turn, 0), order_own(0, j)))
    for j in range(len(spans)):
        last = max(
            (mid - 1) * chunks + sequence[c % 2].index(c) for c in range(j * joined, (j + 1) * joined)
        )
        todo.append((last, late_own(j)))
        todo.append((last, order_own(1, j)))
        todo.append((last + 1, late_peer(j)))

    slot = 0
    for d in range(1, mid + 1):
        for i in range(chunks):
            moved = False
            for side in range(2):
                c = sequence[side][i]
                if d <= reach(c, side):
                    moved = True
                    ring_copy(c, d - 1, side).wait_recv()
                    if d < reach(c, side):
                        ring_copy(c, d, side).start()
                    pair_copy(c, spot(d, side), core).start()
            if moved and todo and todo[0][0] <= slot:
                todo.pop(0)[1]()
            slot += 1
    for _, run in todo:
        run()

    size = k_send.shape[1]
    count = size // per
    near = me // mid
    local = me % mid
    pieces = []
    for b in (1 - near, near):
        for s in range(half // size):
            pieces.append((b, s))

    def piece_rows(b, s):
        return pl.ds(pl.multiple_of(b * half + s * size, size), size)

    def half_copy(i):
        return pltpu.make_async_remote_copy(
            src_ref=k_send.at[i], dst_ref=k_peer.at[i], send_sem=half_send.at[i],
            recv_sem=half_recv.at[i], device_id={"gvec": peer}, device_id_type=MESH,
        )

    def out_copy(target, slot):
        return pltpu.make_async_remote_copy(
            src_ref=k_red.at[pl.ds(pl.multiple_of(target * per, per), per), :],
            dst_ref=rows_in.at[me], send_sem=out_send.at[slot], recv_sem=out_recv.at[me],
            device_id={"freq": target}, device_id_type=MESH,
        )

    for i, (b, s) in enumerate(pieces):
        k_send[i] = jnp.dot(e_buf[piece_rows(b, s), :], p_buf[peer], preferred_element_type=F32)
        half_copy(i).start()
    for i, (b, s) in enumerate(pieces):
        k_own[i] = jnp.dot(e_buf[piece_rows(b, s), :], p_buf[core], preferred_element_type=F32)
    sent = 0
    targets = []
    for i, (b, s) in enumerate(pieces):
        half_copy(i).wait_recv()
        k_red[piece_rows(b, s), :] = (k_own[i] + k_peer[i]).astype(BF16)
        for t in range(count):
            target = b * mid + s * count + (local + t) % count
            if i < half // size:
                out_copy(target, sent).start()
            else:
                @pl.when(target != me)
                def _():
                    out_copy(target, sent).start()
            targets.append(target)
            sent += 1
    rows_in[me] = k_red[mine, :]

    def arrived(t):
        source = near * mid + (local + t) % mid if t < mid else (1 - near) * mid + (local + t) % mid
        pltpu.make_async_remote_copy(
            src_ref=rows_in.at[source], dst_ref=rows_in.at[source],
            send_sem=out_send.at[0], recv_sem=out_recv.at[source],
            device_id={"freq": source}, device_id_type=MESH,
        ).wait_recv()
        return source

    def weighted(o, sources):
        return sum(quad_table[quad_index[o, f]] * rows_in[f].astype(F32) for f in sources)

    sources = [me]
    for t in range(1, mid):
        sources.append(arrived(t))
    for o in range(out.shape[0]):
        out[o] = weighted(o, sources)
    sources = [arrived(t) for t in range(mid, n)]
    for o in range(out.shape[0]):
        out[o] = out[o] + weighted(o, sources)

    for c in range(chunks):
        for side in range(2):
            for d in range(reach(c, side)):
                ring_copy(c, d, side).wait_send()
        for at in range(1, n):
            pair_copy(c, at, core).wait_send()
    own_pair(core).wait_send()
    for i in range(len(pieces)):
        half_copy(i).wait_send()
    for slot, target in enumerate(targets):
        if slot < mid:
            out_copy(target, slot).wait_send()
        else:
            @pl.when(target != me)
            def _():
                out_copy(target, slot).wait_send()


def body(n, screened, densities, pair_order, quad_index, quad_table):
    rows, per = densities.shape
    pairs = n * per
    half = pairs // 2
    mid = n // 2
    chunks = next(c for c in (4, 3, 2, 1) if rows % (c * 128) == 0 or c == 1)
    width = rows // chunks
    size = half // 2 if mid % 2 == 0 and (half // 2) % 16 == 0 else half
    count = half // size * 2
    energies = quad_index.shape[0]
    dma = pltpu.SemaphoreType.DMA
    hbm = pl.BlockSpec(memory_space=pl.ANY)
    vmem = pl.BlockSpec(memory_space=pltpu.VMEM)
    smem = pl.BlockSpec(memory_space=pltpu.SMEM)
    return pl.pallas_call(
        functools.partial(kernel, n, chunks),
        out_shape=pltpu.VMEM((energies, per, half), F32),
        in_specs=[hbm, hbm, vmem, smem, smem],
        out_specs=vmem,
        scratch_shapes=[
            pltpu.VMEM((2, rows, rows), BF16),
            pltpu.VMEM((2, pairs, rows), BF16),
            pltpu.VMEM((pairs, rows), BF16),
            pltpu.VMEM((2, rows, half), F32),
            pltpu.VMEM((2, rows, half), BF16),
            pltpu.VMEM((2, rows, half), BF16),
            pltpu.VMEM((pairs, pairs), BF16),
            pltpu.VMEM((pairs, pairs), BF16),
            pltpu.VMEM((count, size, half), F32),
            pltpu.VMEM((count, size, half), F32),
            pltpu.VMEM((count, size, half), F32),
            pltpu.VMEM((pairs, half), BF16),
            pltpu.VMEM((n, per, half), BF16),
            dma((1,)), dma((2,)),
            dma((chunks, n)), dma((chunks, n)),
            dma((1,)), dma((1,)),
            dma((chunks, n)), dma((chunks, n)),
            dma((count,)), dma((count,)), dma((n,)), dma((n,)),
        ],
        compiler_params=pltpu.CompilerParams(
            collective_id=0, has_side_effects=True, vmem_limit_bytes=56 * 1024 * 1024
        ),
    )(screened, densities.T, pair_order[None, :], quad_index, quad_table)


def solution(mesh):
    placed = (P(("groups", "freq"), "gvec", None), P(("groups", "gvec"), "freq"), P(), P(), P())
    return jax.shard_map(
        functools.partial(body, mesh.shape["freq"]), mesh=mesh, in_specs=placed,
        out_specs=P("groups", "freq", "gvec"), check_vma=False,
    )
```

time: 47.6 us -> 40.5 us (0.85)
  Pallas kernels: 45.7 us -> 39.6 us
  local copies, waits for them, and re-layouts: 1.67 us -> 0.71 us
    pallas_call x1, Pallas kernels: 45.7 us -> 39.6 us  [body(): pl.pallas_call(functools.partial(kernel, n, chunks), out_shape=pltpu.VMEM...]
    unnamed x1, local copies, waits for them, and re-layouts: 1.67 us -> 0.71 us
where the time goes in v1:
time: 40.5 us; the launch traced here: 40.3 us
  Pallas kernels  39.6 us (98%)
  local copies, waits for them, and re-layouts  0.71 us (2%)
    pallas_call x1, Pallas kernels, body(): pl.pallas_call(functools.partial(kernel, n, chunks), out_shape=pltpu.VMEM...  39.6 us

profile of v1, /device:TPU:0, one launch (start us, length us, event | category | flops | bytes accessed | tf_op | source)
XLA Modules:
  0.0 40.3 jit_solution(15954730227740192356)
XLA Ops:
  0.0 39.6 %shard_map.55 = f32[4,64,256]{2,1,0:T(8,128)S(1)} custom-call(bf16[1,1536,3072]{2,1,0:T(8,128)(2,1)} %screened.1, bf16[64,1536]{1,0:T(8,128)(2,1)} %bitcast.2, s32[1,512]{1,0:T(1,128)} %bitcast.3, s32[4,8]{1,0:T(4,128)} %quad_index.1, f32[64]{0:T(128)} %quad_table.1), custom_call_target="tpu_custom_call" | custom-call | tf_op jit(solution)/shard_map/pallas_call | solution.py:332
  39.6 0.7 %copy.7 = f32[4,64,256]{2,1,0:T(8,128)} copy(f32[4,64,256]{2,1,0:T(8,128)S(1)} %shard_map.55) | data formatting | bytes 524288

commit v2 on v1

--- a/solution.py
+++ b/solution.py
@@ -146,38 +146,33 @@
             else:
                 p_buf[h, at, :] = (part + pa_buf[h, at, :].astype(F32)).astype(BF16)
 
-    def early(j, at):
+    def early(j):
         def run():
             have_w()
             have(0, j)
-            total = term(0, j, 0, at) + term(0, j, 1, at)
-            if j > 0:
-                total = total + acc[0, at, :]
-            if j < len(spans) - 1:
-                acc[0, at, :] = total
-            else:
-                turned(0, at, total)
+            for at in tiles:
+                total = term(0, j, 0, at) + term(0, j, 1, at)
+                if j > 0:
+                    total = total + acc[0, at, :]
+                if j < len(spans) - 1:
+                    acc[0, at, :] = total
+                else:
+                    turned(0, at, total)
         return run
 
-    def late_own(j):
+    def late(j):
         def run():
             have_w()
+            if j > 0:
+                have(1, j - 1)
             for at in tiles:
-                total = term(1, j, core, at)
+                parts = []
                 if j > 0:
-                    total = total + acc[1, at, :]
-                acc[1, at, :] = total
-        return run
-
-    def late_peer(j):
-        def run():
-            have(1, j)
-            for at in tiles:
-                total = acc[1, at, :] + term(1, j, peer, at)
-                if j < len(spans) - 1:
-                    acc[1, at, :] = total
+                    parts = [acc[1, at, :], term(1, j - 1, peer, at)]
+                if j < len(spans):
+                    acc[1, at, :] = sum(parts + [term(1, j, core, at)])
                 else:
-                    turned(1, at, total)
+                    turned(1, at, sum(parts))
         return run
 
     def order_own(g, j):
@@ -190,26 +185,22 @@
             e_buf[:, spans[j]] = part.astype(BF16)
         return run
 
-    def arrival(j, d, side):
+    def arrival(j, d):
         return max(
             (d - 1) * chunks + sequence[side].index(c)
-            for c in range(j * joined, (j + 1) * joined) if c % 2 == side or d < mid
-        )
-
+            for c in range(j * joined, (j + 1) * joined) for side in range(2)
+            if d < mid or c % 2 == side
+        )
+
+    turn = (mid + 1) // 2
     todo = []
-    turn = mid // 2
     for j in range(len(spans)):
-        for at in tiles:
-            todo.append((arrival(j, turn, 0) + 1, early(j, at)))
+        todo.append((arrival(j, turn) + 1 + j, early(j)))
+        todo.append((arrival(j, turn) + 2 + j, order_own(0, j)))
     for j in range(len(spans)):
-        todo.append((arrival(j, turn, 0), order_own(0, j)))
-    for j in range(len(spans)):
-        last = max(
-            (mid - 1) * chunks + sequence[c % 2].index(c) for c in range(j * joined, (j + 1) * joined)
-        )
-        todo.append((last, late_own(j)))
-        todo.append((last, order_own(1, j)))
-        todo.append((last + 1, late_peer(j)))
+        todo.append((arrival(j, mid), late(j)))
+        todo.append((arrival(j, mid), order_own(1, j)))
+    todo.append((mid * chunks, late(len(spans))))
 
     slot = 0
     for d in range(1, mid + 1):
@@ -233,10 +224,11 @@
     count = size // per
     near = me // mid
     local = me % mid
+    parts = half // size
     pieces = []
     for b in (1 - near, near):
-        for s in range(half // size):
-            pieces.append((b, s))
+        for s in range(parts):
+            pieces.append((b, s + b * (parts - 1 - 2 * s)))
 
     def piece_rows(b, s):
         return pl.ds(pl.multiple_of(b * half + s * size, size), size)
@@ -254,26 +246,31 @@
             device_id={"freq": target}, device_id_type=MESH,
         )
 
-    for i, (b, s) in enumerate(pieces):
-        k_send[i] = jnp.dot(e_buf[piece_rows(b, s), :], p_buf[peer], preferred_element_type=F32)
-        half_copy(i).start()
-    for i, (b, s) in enumerate(pieces):
-        k_own[i] = jnp.dot(e_buf[piece_rows(b, s), :], p_buf[core], preferred_element_type=F32)
+    far = half // size
+    for stage in (range(far), range(far, len(pieces))):
+        for i in stage:
+            k_send[i] = jnp.dot(e_buf[piece_rows(*pieces[i]), :], p_buf[peer], preferred_element_type=F32)
+            half_copy(i).start()
+        for i in stage:
+            k_own[i] = jnp.dot(e_buf[piece_rows(*pieces[i]), :], p_buf[core], preferred_element_type=F32)
     sent = 0
     targets = []
     for i, (b, s) in enumerate(pieces):
         half_copy(i).wait_recv()
         k_red[piece_rows(b, s), :] = (k_own[i] + k_peer[i]).astype(BF16)
-        for t in range(count):
-            target = b * mid + s * count + (local + t) % count
-            if i < half // size:
-                out_copy(target, sent).start()
-            else:
-                @pl.when(target != me)
-                def _():
+        if i % parts == parts - 1:
+            for t in range(mid):
+                first, second = t // parts, t % parts
+                place_s = pieces[i - parts + 1 + second][1]
+                target = b * mid + place_s * count + first
+                if i < parts:
                     out_copy(target, sent).start()
-            targets.append(target)
-            sent += 1
+                else:
+                    @pl.when(target != me)
+                    def _():
+                        out_copy(target, sent).start()
+                targets.append(target)
+                sent += 1
     rows_in[me] = k_red[mine, :]
 
     def arrived(t):

time: 40.5 us -> 38.7 us (0.956)
  Pallas kernels: 39.6 us -> 37.8 us
    pallas_call x1, Pallas kernels: 39.6 us -> 37.8 us  [body(): pl.pallas_call(functools.partial(kernel, n, chunks), out_shape=pltpu.VMEM...]
where the time goes in v2:
time: 38.7 us; the launch traced here: 38.5 us
  Pallas kernels  37.8 us (98%)
  local copies, waits for them, and re-layouts  0.71 us (2%)
    pallas_call x1, Pallas kernels, body(): pl.pallas_call(functools.partial(kernel, n, chunks), out_shape=pltpu.VMEM...  37.8 us

profile of v2, /device:TPU:0, one launch (start us, length us, event | category | flops | bytes accessed | tf_op | source)
XLA Modules:
  0.0 38.5 jit_solution(4052711779495612552)
XLA Ops:
  0.0 37.8 %shard_map.55 = f32[4,64,256]{2,1,0:T(8,128)S(1)} custom-call(bf16[1,1536,3072]{2,1,0:T(8,128)(2,1)} %screened.1, bf16[64,1536]{1,0:T(8,128)(2,1)} %bitcast.2, s32[1,512]{1,0:T(1,128)} %bitcast.3, s32[4,8]{1,0:T(4,128)} %quad_index.1, f32[64]{0:T(128)} %quad_table.1), custom_call_target="tpu_custom_call" | custom-call | tf_op jit(solution)/shard_map/pallas_call | solution.py:329
  37.8 0.7 %copy.7 = f32[4,64,256]{2,1,0:T(8,128)} copy(f32[4,64,256]{2,1,0:T(8,128)S(1)} %shard_map.55) | data formatting | bytes 524288

commit v3 on v2

--- a/solution.py
+++ b/solution.py
@@ -137,14 +137,13 @@
 
     def turned(g, at, total):
         total = total.astype(BF16)
+        both = jnp.dot(total, order_rows[groups[g], :], preferred_element_type=F32).astype(BF16)
         for h in range(2):
-            part = jnp.dot(
-                total, order_rows[groups[g], h * half:(h + 1) * half], preferred_element_type=F32
-            )
+            part = both[:, h * half:(h + 1) * half]
             if g == 0:
-                pa_buf[h, at, :] = part.astype(BF16)
+                pa_buf[h, at, :] = part
             else:
-                p_buf[h, at, :] = (part + pa_buf[h, at, :].astype(F32)).astype(BF16)
+                p_buf[h, at, :] = part + pa_buf[h, at, :]
 
     def early(j):
         def run():
@@ -216,6 +215,8 @@
                     pair_copy(c, spot(d, side), core).start()
             if moved and todo and todo[0][0] <= slot:
                 todo.pop(0)[1]()
+                if d == mid and todo and todo[0][0] <= slot - i:
+                    todo.pop(0)[1]()
             slot += 1
     for _, run in todo:
         run()
@@ -226,9 +227,9 @@
     local = me % mid
     parts = half // size
     pieces = []
-    for b in (1 - near, near):
+    for b in range(2):
         for s in range(parts):
-            pieces.append((b, s + b * (parts - 1 - 2 * s)))
+            pieces.append((b, s))
 
     def piece_rows(b, s):
         return pl.ds(pl.multiple_of(b * half + s * size, size), size)
@@ -247,30 +248,36 @@
         )
 
     far = half // size
-    for stage in (range(far), range(far, len(pieces))):
-        for i in stage:
-            k_send[i] = jnp.dot(e_buf[piece_rows(*pieces[i]), :], p_buf[peer], preferred_element_type=F32)
-            half_copy(i).start()
-        for i in stage:
-            k_own[i] = jnp.dot(e_buf[piece_rows(*pieces[i]), :], p_buf[core], preferred_element_type=F32)
-    sent = 0
+    def emit(i):
+        k_send[i] = jnp.dot(e_buf[piece_rows(*pieces[i]), :], p_buf[peer], preferred_element_type=F32)
+        half_copy(i).start()
+
+    def keep(i):
+        k_own[i] = jnp.dot(e_buf[piece_rows(*pieces[i]), :], p_buf[core], preferred_element_type=F32)
+
     targets = []
-    for i, (b, s) in enumerate(pieces):
+
+    def finish(i):
+        b, s = pieces[i]
         half_copy(i).wait_recv()
         k_red[piece_rows(b, s), :] = (k_own[i] + k_peer[i]).astype(BF16)
-        if i % parts == parts - 1:
-            for t in range(mid):
-                first, second = t // parts, t % parts
-                place_s = pieces[i - parts + 1 + second][1]
-                target = b * mid + place_s * count + first
-                if i < parts:
-                    out_copy(target, sent).start()
-                else:
-                    @pl.when(target != me)
-                    def _():
-                        out_copy(target, sent).start()
-                targets.append(target)
-                sent += 1
+        for t in range(count):
+            target = b * mid + s * count + t
+            slot = len(targets)
+
+            @pl.when(target != me)
+            def _():
+                out_copy(target, slot).start()
+
+            targets.append(target)
+
+    last = len(pieces)
+    for i in range(last + 2):
+        if i < last:
+            emit(i)
+            keep(i)
+        if i >= 2:
+            finish(i - 2)
     rows_in[me] = k_red[mine, :]
 
     def arrived(t):
@@ -304,12 +311,9 @@
     for i in range(len(pieces)):
         half_copy(i).wait_send()
     for slot, target in enumerate(targets):
-        if slot < mid:
+        @pl.when(target != me)
+        def _():
             out_copy(target, slot).wait_send()
-        else:
-            @pl.when(target != me)
-            def _():
-                out_copy(target, slot).wait_send()
 
 
 def body(n, screened, densities, pair_order, quad_index, quad_table):

time: 38.7 us -> 38 us (0.982)
  Pallas kernels: 37.8 us -> 37.1 us
    pallas_call x1, Pallas kernels: 37.8 us -> 37.1 us  [body(): pl.pallas_call(functools.partial(kernel, n, chunks), out_shape=pltpu.VMEM...]
where the time goes in v3:
time: 38 us; the launch traced here: 37.8 us
  Pallas kernels  37.1 us (98%)
  local copies, waits for them, and re-layouts  0.71 us (2%)
    pallas_call x1, Pallas kernels, body(): pl.pallas_call(functools.partial(kernel, n, chunks), out_shape=pltpu.VMEM...  37.1 us

profile of v3, /device:TPU:0, one launch (start us, length us, event | category | flops | bytes accessed | tf_op | source)
XLA Modules:
  0.0 37.8 jit_solution(16578320355911081410)
XLA Ops:
  0.0 37.1 %shard_map.55 = f32[4,64,256]{2,1,0:T(8,128)S(1)} custom-call(bf16[1,1536,3072]{2,1,0:T(8,128)(2,1)} %screened.1, bf16[64,1536]{1,0:T(8,128)(2,1)} %bitcast.2, s32[1,512]{1,0:T(1,128)} %bitcast.3, s32[4,8]{1,0:T(4,128)} %quad_index.1, f32[64]{0:T(128)} %quad_table.1), custom_call_target="tpu_custom_call" | custom-call | tf_op jit(solution)/shard_map/pallas_call | solution.py:333
  37.1 0.7 %copy.7 = f32[4,64,256]{2,1,0:T(8,128)} copy(f32[4,64,256]{2,1,0:T(8,128)S(1)} %shard_map.55) | data formatting | bytes 524288

commit v4 on v3

--- a/solution.py
+++ b/solution.py
@@ -15,7 +15,7 @@
 
 def kernel(
     n, chunks, screened, dens, order, quad_index, quad_table, out,
-    w_buf, x_buf, e_buf, acc, pa_buf, p_buf, perm, order_rows, k_send, k_peer, k_own, k_red, rows_in,
+    w_buf, x_buf, e_buf, acc, t_buf, pa_buf, p_buf, perm, order_rows, k_send, k_peer, k_own, k_red, rows_in,
     own_sem, w_sem, ring_send, ring_recv, own_send, own_recv, pair_send, pair_recv,
     half_send, half_recv, out_send, out_recv,
 ):
@@ -135,15 +135,17 @@
             w_buf[h, at, spans[j]], x_buf[h, groups[g], spans[j]], NT, preferred_element_type=F32
         )
 
-    def turned(g, at, total):
-        total = total.astype(BF16)
-        both = jnp.dot(total, order_rows[groups[g], :], preferred_element_type=F32).astype(BF16)
-        for h in range(2):
-            part = both[:, h * half:(h + 1) * half]
-            if g == 0:
-                pa_buf[h, at, :] = part
-            else:
-                p_buf[h, at, :] = part + pa_buf[h, at, :]
+    def turned(g):
+        for at in tiles:
+            both = jnp.dot(
+                t_buf[g, at, :], order_rows[groups[g], :], preferred_element_type=F32
+            ).astype(BF16)
+            for h in range(2):
+                part = both[:, h * half:(h + 1) * half]
+                if g == 0:
+                    pa_buf[h, at, :] = part
+                else:
+                    p_buf[h, at, :] = part + pa_buf[h, at, :]
 
     def early(j):
         def run():
@@ -156,7 +158,9 @@
                 if j < len(spans) - 1:
                     acc[0, at, :] = total
                 else:
-                    turned(0, at, total)
+                    t_buf[0, at, :] = total.astype(BF16)
+            if j == len(spans) - 1:
+                turned(0)
         return run
 
     def late(j):
@@ -171,7 +175,9 @@
                 if j < len(spans):
                     acc[1, at, :] = sum(parts + [term(1, j, core, at)])
                 else:
-                    turned(1, at, sum(parts))
+                    t_buf[1, at, :] = sum(parts).astype(BF16)
+            if j == len(spans):
+                turned(1)
         return run
 
     def order_own(g, j):
@@ -280,27 +286,6 @@
             finish(i - 2)
     rows_in[me] = k_red[mine, :]
 
-    def arrived(t):
-        source = near * mid + (local + t) % mid if t < mid else (1 - near) * mid + (local + t) % mid
-        pltpu.make_async_remote_copy(
-            src_ref=rows_in.at[source], dst_ref=rows_in.at[source],
-            send_sem=out_send.at[0], recv_sem=out_recv.at[source],
-            device_id={"freq": source}, device_id_type=MESH,
-        ).wait_recv()
-        return source
-
-    def weighted(o, sources):
-        return sum(quad_table[quad_index[o, f]] * rows_in[f].astype(F32) for f in sources)
-
-    sources = [me]
-    for t in range(1, mid):
-        sources.append(arrived(t))
-    for o in range(out.shape[0]):
-        out[o] = weighted(o, sources)
-    sources = [arrived(t) for t in range(mid, n)]
-    for o in range(out.shape[0]):
-        out[o] = out[o] + weighted(o, sources)
-
     for c in range(chunks):
         for side in range(2):
             for d in range(reach(c, side)):
@@ -310,6 +295,29 @@
     own_pair(core).wait_send()
     for i in range(len(pieces)):
         half_copy(i).wait_send()
+
+    def arrived(t):
+        source = near * mid + (local + t) % mid if t < mid else (1 - near) * mid + (local + t) % mid
+        pltpu.make_async_remote_copy(
+            src_ref=rows_in.at[source], dst_ref=rows_in.at[source],
+            send_sem=out_send.at[0], recv_sem=out_recv.at[source],
+            device_id={"freq": source}, device_id_type=MESH,
+        ).wait_recv()
+        return source
+
+    def weighted(o, sources):
+        return sum(quad_table[quad_index[o, f]] * rows_in[f].astype(F32) for f in sources)
+
+    sources = [me]
+    for t in range(1, mid):
+        sources.append(arrived(t))
+    for o in range(out.shape[0]):
+        out[o] = weighted(o, sources)
+    for t in range(mid, n, 2):
+        sources = [arrived(t), arrived(t + 1)]
+        for o in range(out.shape[0]):
+            out[o] = out[o] + weighted(o, sources)
+
     for slot, target in enumerate(targets):
         @pl.when(target != me)
         def _():
@@ -342,6 +350,7 @@
             pltpu.VMEM((2, rows, half), F32),
             pltpu.VMEM((2, rows, half), BF16),
             pltpu.VMEM((2, rows, half), BF16),
+            pltpu.VMEM((2, rows, half), BF16),
             pltpu.VMEM((pairs, pairs), BF16),
             pltpu.VMEM((pairs, pairs), BF16),
             pltpu.VMEM((count, size, half), F32),

time: 38 us -> 36.3 us (0.955)
  Pallas kernels: 37.1 us -> 35.4 us
    pallas_call x1, Pallas kernels: 37.1 us -> 35.4 us  [body(): pl.pallas_call(functools.partial(kernel, n, chunks), out_shape=pltpu.VMEM...]
where the time goes in v4:
time: 36.3 us; the launch traced here: 36.2 us
  Pallas kernels  35.4 us (98%)
  local copies, waits for them, and re-layouts  0.71 us (2%)
    pallas_call x1, Pallas kernels, body(): pl.pallas_call(functools.partial(kernel, n, chunks), out_shape=pltpu.VMEM...  35.4 us

profile of v4, /device:TPU:0, one launch (start us, length us, event | category | flops | bytes accessed | tf_op | source)
XLA Modules:
  0.0 36.2 jit_solution(4776640331711111340)
XLA Ops:
  0.0 35.4 %shard_map.55 = f32[4,64,256]{2,1,0:T(8,128)S(1)} custom-call(bf16[1,1536,3072]{2,1,0:T(8,128)(2,1)} %screened.1, bf16[64,1536]{1,0:T(8,128)(2,1)} %bitcast.2, s32[1,512]{1,0:T(1,128)} %bitcast.3, s32[4,8]{1,0:T(4,128)} %quad_index.1, f32[64]{0:T(128)} %quad_table.1), custom_call_target="tpu_custom_call" | custom-call | tf_op jit(solution)/shard_map/pallas_call | solution.py:341
  35.5 0.7 %copy.7 = f32[4,64,256]{2,1,0:T(8,128)} copy(f32[4,64,256]{2,1,0:T(8,128)S(1)} %shard_map.55) | data formatting | bytes 524288

commit v5 on v4

--- a/solution.py
+++ b/solution.py
@@ -38,12 +38,12 @@
     left = index_at((place + n - 1) % n)
 
     own_copy = pltpu.make_async_copy(dens, x_buf.at[core, 0:per, :], own_sem.at[0])
-    own_copy.start()
 
     barrier = pltpu.get_barrier_semaphore()
     pl.semaphore_signal(barrier, inc=1, device_id={"freq": left}, device_id_type=MESH)
     pl.semaphore_signal(barrier, inc=1, device_id={"freq": right}, device_id_type=MESH)
     pl.semaphore_signal(barrier, inc=1, device_id={"gvec": peer}, device_id_type=MESH)
+    own_copy.start()
 
     def w_copy(h):
         return pltpu.make_async_copy(
@@ -278,12 +278,12 @@
             targets.append(target)
 
     last = len(pieces)
-    for i in range(last + 2):
+    for i in range(last + 1):
         if i < last:
             emit(i)
             keep(i)
-        if i >= 2:
-            finish(i - 2)
+        if i >= 1:
+            finish(i - 1)
     rows_in[me] = k_red[mine, :]
 
     for c in range(chunks):

time: 36.3 us -> 36.3 us (level)
  no operation moved by 1% of the time
where the time goes in v5:
time: 36.3 us; the launch traced here: 36.1 us
  Pallas kernels  35.4 us (98%)
  local copies, waits for them, and re-layouts  0.71 us (2%)
    pallas_call x1, Pallas kernels, body(): pl.pallas_call(functools.partial(kernel, n, chunks), out_shape=pltpu.VMEM...  35.4 us

profile of v5, /device:TPU:0, one launch (start us, length us, event | category | flops | bytes accessed | tf_op | source)
XLA Modules:
  0.0 36.1 jit_solution(16435657263091177430)
XLA Ops:
  0.0 35.4 %shard_map.55 = f32[4,64,256]{2,1,0:T(8,128)S(1)} custom-call(bf16[1,1536,3072]{2,1,0:T(8,128)(2,1)} %screened.1, bf16[64,1536]{1,0:T(8,128)(2,1)} %bitcast.2, s32[1,512]{1,0:T(1,128)} %bitcast.3, s32[4,8]{1,0:T(4,128)} %quad_index.1, f32[64]{0:T(128)} %quad_table.1), custom_call_target="tpu_custom_call" | custom-call | tf_op jit(solution)/shard_map/pallas_call | solution.py:341
  35.4 0.7 %copy.7 = f32[4,64,256]{2,1,0:T(8,128)} copy(f32[4,64,256]{2,1,0:T(8,128)S(1)} %shard_map.55) | data formatting | bytes 524288
